TPU v7x, 32 devices: a whole 2x2x4 slice. The times are simulated.
32 devices in a mesh: act: 8 (over z, x), rep: 4 (over y, core).
Axes of the slice: x: 2, y: 2, z: 4, core: 2. Of those that a mesh axis runs over, the one named last changes fastest.
Arguments:
- estimated_returns: float32 [512, 16384], P('act', 'rep'), may hold values from -1000 to 1000
- chosen_move_ids: int32 [512, 16384], P('act', 'rep'), may hold values from 0 to 17
- previous_eta: float32 [1], replicated, may hold values from 0.3 to 3
- trust_region_epsilon: float32 [1], replicated, may hold values from 0.02 to 1
Outputs:
- sample_importance: float32 [512, 16384], P('act', 'rep')
- goal_distribution: float32 [18, 16384], P(None, ('rep', 'act'))
- new_temperature: float32 [1], replicated
All inputs are finite; a program needn't handle non-finite values.
Results may differ from a plain program's by a relative error of at most 0.0003.
Values sent between devices are 32-bit elements; how exact they have to be, the bound alone decides.
A program may use at most 64 MiB of HBM per device.

v0:
```python
import jax
import jax.numpy as jnp
from jax import lax
from jax.sharding import PartitionSpec as P

NACT = 18
ITERS = 3


def summary_figures(centered_returns, lagrange_eta):
    exponential_term = jnp.exp(centered_returns / lagrange_eta)
    partition_total = jnp.sum(exponential_term, axis=0)
    leading_part = jnp.sum(exponential_term * centered_returns, axis=0)
    trailing_part = jnp.sum(exponential_term * centered_returns * centered_returns, axis=0)
    return (exponential_term, partition_total, leading_part, trailing_part)


def within_situation(partition_total, leading_part, trailing_part, lagrange_eta, move_draws):
    entropy_gap = (
        leading_part / (partition_total * lagrange_eta)
        - jnp.log(partition_total)
        + jnp.log(jnp.float32(move_draws))
    )
    mean_first = leading_part / partition_total
    spread = trailing_part / partition_total - mean_first * mean_first
    return (jnp.sum(entropy_gap), jnp.sum(spread))


def gradient_step(lagrange_eta, ceiling_term, aggregate_relative_entropy, aggregate_deviation):
    change_amount = (
        (ceiling_term - aggregate_relative_entropy)
        * lagrange_eta
        / (1.0 + aggregate_deviation / lagrange_eta)
    )
    return lagrange_eta * jnp.exp(-jnp.tanh(change_amount))


def per_action(probs, ids_block):
    return jnp.stack([jnp.sum(jnp.where(ids_block == k, probs, 0.0), axis=0) for k in range(NACT)])


def scatter_target(probs, ids_block):
    return lax.psum_scatter(per_action(probs, ids_block), "act", scatter_dimension=1, tiled=True)


def on_device(estimated_returns, chosen_move_ids, previous_eta, trust_region_epsilon):
    lagrange_eta = previous_eta[0]
    ceiling_term = trust_region_epsilon[0]
    move_draws = estimated_returns.shape[0] * lax.axis_size("act")
    q_rows = lax.all_to_all(estimated_returns, "act", split_axis=1, concat_axis=0, tiled=True)
    tally_number = q_rows.shape[1] * lax.axis_size("act") * lax.axis_size("rep")
    centered_returns = q_rows - jnp.max(q_rows, axis=0, keepdims=True)
    for step in range(ITERS):
        exponential_term, partition_total, leading_part, trailing_part = summary_figures(
            centered_returns, lagrange_eta
        )
        shard_divergence, shard_value_spread = within_situation(
            partition_total, leading_part, trailing_part, lagrange_eta, move_draws
        )
        aggregate_relative_entropy, aggregate_deviation = lax.psum(
            (shard_divergence, shard_value_spread), ("act", "rep")
        )
        lagrange_eta = gradient_step(
            lagrange_eta,
            ceiling_term,
            aggregate_relative_entropy / tally_number,
            aggregate_deviation / tally_number,
        )
    exponential_term, partition_total, leading_part, trailing_part = summary_figures(
        centered_returns, lagrange_eta
    )
    probs_rows = exponential_term / partition_total
    sample_importance = lax.all_to_all(
        move_draws * probs_rows, "act", split_axis=0, concat_axis=1, tiled=True
    )
    goal_distribution = scatter_target(sample_importance / jnp.float32(move_draws), chosen_move_ids)
    return (sample_importance, goal_distribution, jnp.reshape(lagrange_eta, (1,)))


def solution(mesh):
    in_specs = (P("act", "rep"), P("act", "rep"), P(), P())
    out_specs = (P("act", "rep"), P(None, ("rep", "act")), P())
    return jax.shard_map(
        on_device, mesh=mesh, in_specs=in_specs, out_specs=out_specs, check_vma=False
    )
```

profile of v0, /device:TPU:0, one launch (start us, length us, event | category | flops | bytes accessed | tf_op | source)
XLA Modules:
  0.0 275.7 jit_solution(3576206588471246463)
XLA Ops:
  7.2 2.3 copy.12
  9.4 7.3 %all-to-all-start = ((f32[64,8,512]{2,0,1:T(8,128)}), f32[64,8,512]{2,0,1:T(8,128)S(1)}, u32[]{:S(2)}, u32[]{:S(2)}) async-start(f32[64,8,512]{2,0,1:T(8,128)} %bitcast.86), calls=%async_computation | async-start | bytes 2097152 | tf_op jit(solution)/shard_map/all_to_all | solution.py:50
  16.7 0.0 reduce-scatter.2.cloned.1.call-start
  18.1 24.4 %all-to-all-done = f32[64,8,512]{2,0,1:T(8,128)S(1)} async-done(((f32[64,8,512]{2,0,1:T(8,128)}), f32[64,8,512]{2,0,1:T(8,128)S(1)}, u32[]{:S(2)}, u32[]{:S(2)}) %all-to-all-start) | async-done | bytes 1048608 | tf_op jit(solution)/shard_map/all_to_all | solution.py:50
  42.5 0.1 reduce_max.9
  42.6 0.3 fusion.1
  42.9 0.7 subtract_reduce_fusion.2
  43.6 38.0 %all-reduce.2 = (f32[]{:T(128)}, f32[]{:T(128)}) all-reduce(f32[]{:T(128)} %get-tuple-element.35, f32[]{:T(128)} %get-tuple-element.34), channel_id=1, replica_groups=mesh['act'=8,'rep'=4] {'act','rep'}, use_global_device_ids=true, to_apply=%region_4.0 | all-reduce | flops 2 | bytes 16 | tf_op jit(solution)/shard_map/psum | solution.py:60
  83.0 0.3 fusion.3
  83.3 0.6 subtract_reduce_fusion.1
  84.0 41.8 %all-reduce.1 = (f32[]{:T(128)}, f32[]{:T(128)}) all-reduce(f32[]{:T(128)} %get-tuple-element.33, f32[]{:T(128)} %get-tuple-element.32), channel_id=1, replica_groups=mesh['act'=8,'rep'=4] {'act','rep'}, use_global_device_ids=true, to_apply=%region_11.0 | all-reduce | flops 2 | bytes 16 | tf_op jit(solution)/shard_map/psum | solution.py:60
  127.2 0.3 fusion.5
  127.6 0.6 subtract_reduce_fusion
  128.2 39.7 %all-reduce = (f32[]{:T(128)}, f32[]{:T(128)}) all-reduce(f32[]{:T(128)} %get-tuple-element.31, f32[]{:T(128)} %get-tuple-element.30), channel_id=1, replica_groups=mesh['act'=8,'rep'=4] {'act','rep'}, use_global_device_ids=true, to_apply=%region_18.0 | all-reduce | flops 2 | bytes 16 | tf_op jit(solution)/shard_map/psum | solution.py:60
  169.3 0.2 fusion.13
  169.5 0.2 divide_multiply_fusion
  169.8 29.3 %all_to_all.29 = f32[8,64,512]{2,1,0:T(8,128)S(1)} all-to-all(f32[8,64,512]{2,1,0:T(8,128)S(1)} %divide_multiply_fusion), channel_id=1, replica_groups=mesh['act'=8,'rep'=4] {'act'}, dimensions={0} | all-to-all | bytes 2097152 | tf_op jit(solution)/shard_map/all_to_all | solution.py:73
  199.0 0.0 copy-start.1
  199.0 0.1 copy.10
  199.1 0.0 copy-start
  199.1 1.5 copy-done.1
  200.6 2.7 select_reduce_fusion
  203.4 0.0 copy-done
  203.4 2.4 stack.75
  205.7 0.0 reduce-scatter.2.cloned.1.call-update
  205.8 62.0 %reduce-scatter.2.cloned.1.call-done = f32[18,512]{1,0:T(8,128)} async-done(((f32[18,4096]{1,0:T(8,128)}), f32[18,512]{1,0:T(8,128)}) %reduce-scatter.2.cloned.1.call-update) | async-done | bytes 36880 | tf_op jit(solution)/shard_map/reduce_scatter | solution.py:43
Async XLA Ops:
  9.4 33.0 %all-to-all-start = ((f32[64,8,512]{2,0,1:T(8,128)}), f32[64,8,512]{2,0,1:T(8,128)S(1)}, u32[]{:S(2)}, u32[]{:S(2)}) async-start(f32[64,8,512]{2,0,1:T(8,128)} %bitcast.86), calls=%async_computation | async-start | bytes 2097152 | tf_op jit(solution)/shard_map/all_to_all | solution.py:50
  16.7 251.0 %reduce-scatter.2.cloned.1.call-start = ((), (), s32[]{:S(2)}) async-start(), calls=%async_computation.3 | async-start | bytes 442368 | tf_op jit(solution)/shard_map/reduce_scatter | solution.py:43
  199.0 1.6 copy-start.1
  199.1 4.2 %copy-start = (f32[8,8,8,512]{3,2,0,1:T(8,128)}, f32[8,8,8,512]{3,2,0,1:T(8,128)S(1)}, u32[]{:S(2)}) copy-start(f32[8,8,8,512]{3,2,0,1:T(8,128)S(1)} %copy.10) | copy-start | bytes 3145732
Sparse Core Ops, SparseCore 0:
  205.9 61.8 reduce-scatter.1
where the time goes:
time: 277 us; the launch traced here: 276 us
  blocking collectives  149 us (54%)
  waiting for transfers between devices  86.4 us (31%)
  between operations  20.8 us (8%)
  starting transfers between devices  7.32 us (3%)
  local copies, waits for them, and re-layouts  6.25 us (2%)
  other arithmetic  6.15 us (2%)
    psum x3, blocking collectives, on_device(): lax.psum((shard_divergence, shard_value_spread), ('act', 'rep'))  119 us
    reduce_scatter x1, waiting for transfers between devices, scatter_target(): lax.psum_scatter(per_action(probs, ids_block), 'act', scatter_dimension=1...  62 us
    all_to_all x1, blocking collectives, on_device(): lax.all_to_all(move_draws * probs_rows, 'act', split_axis=0, concat_axis=...  29.3 us
    all_to_all x1, waiting for transfers between devices, on_device(): lax.all_to_all(estimated_returns, 'act', split_axis=1, concat_axis=0, til...  24.4 us
    all_to_all x1, starting transfers between devices, on_device(): lax.all_to_all(estimated_returns, 'act', split_axis=1, concat_axis=0, til...  7.28 us
  transfers between devices with their start and end apart: 2, of which 2 were waited for; matrix products, arithmetic and copies ran while one was open for 0% of the time, Pallas kernels for 0%

commit v1 on v0

--- a/solution.py
+++ b/solution.py
@@ -47,7 +47,12 @@
     lagrange_eta = previous_eta[0]
     ceiling_term = trust_region_epsilon[0]
     move_draws = estimated_returns.shape[0] * lax.axis_size("act")
-    q_rows = lax.all_to_all(estimated_returns, "act", split_axis=1, concat_axis=0, tiled=True)
+    q_rows = jnp.concatenate(
+        lax.all_to_all(
+            jnp.stack(jnp.split(estimated_returns, lax.axis_size("act"), axis=1)), "act", 0, 0
+        ),
+        axis=0,
+    )
     tally_number = q_rows.shape[1] * lax.axis_size("act") * lax.axis_size("rep")
     centered_returns = q_rows - jnp.max(q_rows, axis=0, keepdims=True)
     for step in range(ITERS):

time: 277 us -> 287 us (1.036)
  local copies, waits for them, and re-layouts: 6.25 us -> 16.5 us
    unnamed x4 -> x11, local copies, waits for them, and re-layouts: 1.51 us -> 12.5 us
where the time goes in v1:
time: 287 us; the launch traced here: 286 us
  blocking collectives  149 us (52%)
  waiting for transfers between devices  86.4 us (30%)
  between operations  20.8 us (7%)
  local copies, waits for them, and re-layouts  16.5 us (6%)
  starting transfers between devices  7.32 us (3%)
  other arithmetic  6.15 us (2%)
    psum x3, blocking collectives, on_device(): lax.psum((shard_divergence, shard_value_spread), ('act', 'rep'))  119 us
    reduce_scatter x1, waiting for transfers between devices, scatter_target(): lax.psum_scatter(per_action(probs, ids_block), 'act', scatter_dimension=1...  62 us
    all_to_all x1, blocking collectives, on_device(): lax.all_to_all(move_draws * probs_rows, 'act', split_axis=0, concat_axis=...  29.3 us
    all_to_all x1, waiting for transfers between devices, on_device(): lax.all_to_all(jnp.stack(jnp.split(estimated_returns, lax.axis_size('act'...  24.4 us
    unnamed x11, local copies, waits for them, and re-layouts  12.5 us
    all_to_all x1, starting transfers between devices, on_device(): lax.all_to_all(jnp.stack(jnp.split(estimated_returns, lax.axis_size('act'...  7.28 us
  transfers between devices with their start and end apart: 2, of which 2 were waited for; matrix products, arithmetic and copies ran while one was open for 0% of the time, Pallas kernels for 0%

profile of v1, /device:TPU:0, one launch (start us, length us, event | category | flops | bytes accessed | tf_op | source)
XLA Modules:
  0.0 286.0 jit_solution(5960351318621241986)
XLA Ops:
  7.2 1.6 bitcast_dynamic-update-slice_fusion.7
  8.7 1.6 bitcast_dynamic-update-slice_fusion.6
  10.3 1.6 bitcast_dynamic-update-slice_fusion.5
  11.9 1.6 bitcast_dynamic-update-slice_fusion.4
  13.4 1.6 bitcast_dynamic-update-slice_fusion.3
  15.0 1.6 bitcast_dynamic-update-slice_fusion.2
  16.6 1.6 bitcast_dynamic-update-slice_fusion.1
  18.1 1.6 bitcast_dynamic-update-slice_fusion
  19.7 7.3 %all-to-all-start = ((f32[8,64,512]{2,1,0:T(8,128)}), f32[8,64,512]{2,1,0:T(8,128)S(1)}, u32[]{:S(2)}, u32[]{:S(2)}) async-start(f32[8,64,512]{2,1,0:T(8,128)} %bitcast_dynamic-update-slice_fusion), calls=%async_computation | async-start | bytes 2097152 | tf_op jit(solution)/shard_map/all_to_all | solution.py:51
  27.0 0.0 reduce-scatter.2.cloned.1.call-start
  28.3 24.4 %all-to-all-done = f32[8,64,512]{2,1,0:T(8,128)S(1)} async-done(((f32[8,64,512]{2,1,0:T(8,128)}), f32[8,64,512]{2,1,0:T(8,128)S(1)}, u32[]{:S(2)}, u32[]{:S(2)}) %all-to-all-start) | async-done | bytes 1048608 | tf_op jit(solution)/shard_map/all_to_all | solution.py:51
  52.8 0.1 reduce_max.9
  52.9 0.3 multiply_reduce_fusion.2
  53.2 0.7 subtract_reduce_fusion.2
  53.9 38.0 %all-reduce.2 = (f32[]{:T(128)}, f32[]{:T(128)}) all-reduce(f32[]{:T(128)} %get-tuple-element.35, f32[]{:T(128)} %get-tuple-element.34), channel_id=1, replica_groups=mesh['act'=8,'rep'=4] {'act','rep'}, use_global_device_ids=true, to_apply=%region_4.0 | all-reduce | flops 2 | bytes 16 | tf_op jit(solution)/shard_map/psum | solution.py:65
  93.3 0.3 multiply_reduce_fusion.1
  93.6 0.6 subtract_reduce_fusion.1
  94.2 41.8 %all-reduce.1 = (f32[]{:T(128)}, f32[]{:T(128)}) all-reduce(f32[]{:T(128)} %get-tuple-element.33, f32[]{:T(128)} %get-tuple-element.32), channel_id=1, replica_groups=mesh['act'=8,'rep'=4] {'act','rep'}, use_global_device_ids=true, to_apply=%region_11.0 | all-reduce | flops 2 | bytes 16 | tf_op jit(solution)/shard_map/psum | solution.py:65
  137.5 0.3 multiply_reduce_fusion
  137.8 0.6 subtract_reduce_fusion
  138.4 39.7 %all-reduce = (f32[]{:T(128)}, f32[]{:T(128)}) all-reduce(f32[]{:T(128)} %get-tuple-element.31, f32[]{:T(128)} %get-tuple-element.30), channel_id=1, replica_groups=mesh['act'=8,'rep'=4] {'act','rep'}, use_global_device_ids=true, to_apply=%region_18.0 | all-reduce | flops 2 | bytes 16 | tf_op jit(solution)/shard_map/psum | solution.py:65
  179.6 0.2 fusion.3
  179.8 0.2 divide_multiply_fusion
  180.0 29.3 %all_to_all.21 = f32[8,64,512]{2,1,0:T(8,128)S(1)} all-to-all(f32[8,64,512]{2,1,0:T(8,128)S(1)} %divide_multiply_fusion), channel_id=1, replica_groups=mesh['act'=8,'rep'=4] {'act'}, dimensions={0} | all-to-all | bytes 2097152 | tf_op jit(solution)/shard_map/all_to_all | solution.py:78
  209.3 0.0 copy-start.1
  209.3 0.1 copy.8
  209.4 0.0 copy-start
  209.4 1.5 copy-done.1
  210.9 2.7 select_reduce_fusion
  213.6 0.0 copy-done
  213.6 2.4 stack.111
  216.0 0.0 reduce-scatter.2.cloned.1.call-update
  216.0 62.0 %reduce-scatter.2.cloned.1.call-done = f32[18,512]{1,0:T(8,128)} async-done(((f32[18,4096]{1,0:T(8,128)}), f32[18,512]{1,0:T(8,128)}) %reduce-scatter.2.cloned.1.call-update) | async-done | bytes 36880 | tf_op jit(solution)/shard_map/reduce_scatter | solution.py:43
Async XLA Ops:
  19.7 33.0 %all-to-all-start = ((f32[8,64,512]{2,1,0:T(8,128)}), f32[8,64,512]{2,1,0:T(8,128)S(1)}, u32[]{:S(2)}, u32[]{:S(2)}) async-start(f32[8,64,512]{2,1,0:T(8,128)} %bitcast_dynamic-update-slice_fusion), calls=%async_computation | async-start | bytes 2097152 | tf_op jit(solution)/shard_map/all_to_all | solution.py:51
  27.0 251.0 %reduce-scatter.2.cloned.1.call-start = ((), (), s32[]{:S(2)}) async-start(), calls=%async_computation.3 | async-start | bytes 442368 | tf_op jit(solution)/shard_map/reduce_scatter | solution.py:43
  209.3 1.6 copy-start.1
  209.4 4.2 %copy-start = (f32[8,8,8,512]{3,2,0,1:T(8,128)}, f32[8,8,8,512]{3,2,0,1:T(8,128)S(1)}, u32[]{:S(2)}) copy-start(f32[8,8,8,512]{3,2,0,1:T(8,128)S(1)} %copy.8) | copy-start | bytes 3145732
Sparse Core Ops, SparseCore 0:
  216.1 61.8 reduce-scatter.1
